TPU v7x, 32 devices: a whole 2x2x4 slice. The times are simulated.
32 devices in a mesh: gx: 4 (over y, x), gy: 4 (over z), gz: 2 (over core).
Axes of the slice: x: 2, y: 2, z: 4, core: 2. Of those that a mesh axis runs over, the one named last changes fastest.
Arguments:
- fields: bfloat16 [4096, 2048], P(('gx', 'gy', 'gz')), may hold values from -6 to 6
- coordinates: float32 [3, 524288], P(None, ('gx', 'gy', 'gz')), may hold values from -1 to 1
- element_rank: int32 [524288, 1], P(('gx', 'gy', 'gz')), may hold values from 0 to 31; in each aligned block of 16384 rows (0 to 16383, 16384 to 32767, ...) at most 640 rows name the same one
- element_slot: int32 [524288], P(('gx', 'gy', 'gz')), may hold values from 0 to 127
Outputs:
- samples: float32 [4, 524288], P(None, ('gx', 'gy', 'gz'))
Inputs may be any that keep to these rules, and one draw needn't show every extreme that they name: `element_rank`: among the probes of one device no rank is named by more than 640 probes, and in some devices' blocks one rank is named by exactly 640.
All inputs are finite; a program needn't handle non-finite values.
Results may differ from a plain program's by a relative error of at most 0.0024.
Values sent between devices are 32-bit elements; how exact they have to be, the bound alone decides.
No kernel may reach another device: no remote copies, remote signals or barrier semaphores. Data moves between devices by JAX's collectives and lax.ppermute only.
A program may use at most 64 MiB of HBM per device.

v0:
```python
import functools
import math

import jax
import jax.numpy as jnp
import numpy as np
from jax import lax
from jax.experimental import pallas as pl
from jax.experimental.pallas import tpu as pltpu
from jax.sharding import PartitionSpec as P

LANES = 128

gll_points = np.array([-1.0,-0.8717401485096066,-0.5917001814331423,-0.2092992179024789,0.2092992179024789,0.5917001814331423,0.8717401485096066,1.0])
gll_scale = np.array([1.0 / np.prod([gll_points[a] - gll_points[b] for b in range(8) if b != a]) for a in range(8)])

def lagrange_rows(coord, scale, node):
    weights = jnp.broadcast_to(scale, node.shape)
    for b in range(8):
        offset = coord - np.float32(gll_points[b])
        weights = weights * jnp.where(node == b, np.float32(1.0), offset)
    return weights

def evaluate_kernel(table_ref, probes_ref, samples_ref, *, step):
    cells = probes_ref.shape[0]
    elements = table_ref.shape[1] // 8
    node = lax.broadcasted_iota(jnp.int32, (8, step), 0)
    scale = jnp.full((8, step), gll_scale[0], jnp.float32)
    for a in range(1, 8):
        scale = jnp.where(node == a, np.float32(gll_scale[a]), scale)
    ids = lax.broadcasted_iota(jnp.int32, (elements, step), 0).astype(jnp.float32).astype(jnp.bfloat16)
    per_step = step // LANES
    for at in range(0, cells, per_step):
        block = jnp.concatenate([probes_ref[at + i] for i in range(per_step)], axis=1)
        weight_r = lagrange_rows(block[0:1], scale, node)
        weight_s = lagrange_rows(block[1:2], scale, node)
        weight_t = lagrange_rows(block[2:3], scale, node)
        slot = jnp.broadcast_to(block[3:4], (elements, step)).astype(jnp.bfloat16)
        mine = slot == ids
        right = []
        for c in range(8):
            w = jnp.broadcast_to(weight_t[c:c + 1], (elements, step)).astype(jnp.bfloat16)
            right.append(jnp.where(mine, w, jnp.zeros_like(w)))
        right = jnp.concatenate(right, axis=0)
        along_t = jnp.dot(table_ref[...], right, preferred_element_type=jnp.float32)
        out = []
        for f in range(4):
            acc = None
            for b in range(8):
                at_b = (f * 8 + b) * 8
                term = along_t[at_b:at_b + 8] * weight_s[b:b + 1]
                acc = term if acc is None else acc + term
            out.append(jnp.sum(acc * weight_r, axis=0, keepdims=True))
        out = jnp.concatenate(out, axis=0)
        for i in range(per_step):
            samples_ref[at + i] = out[:, i * LANES:(i + 1) * LANES]

def evaluate(probes, fields, parts=2, step=256):
    cells = probes.shape[0]
    elements = fields.shape[0]
    table = fields.reshape(elements, 4, 8, 8, 8).transpose(1, 3, 2, 4, 0).reshape(256, 8 * elements)
    spec = pl.BlockSpec((cells // parts, 4, LANES), lambda i: (i, 0, 0))
    n = cells * LANES
    return pl.pallas_call(
        functools.partial(evaluate_kernel, step=step),
        grid=(parts,),
        in_specs=[pl.BlockSpec((256, 8 * elements), lambda i: (0, 0)), spec],
        out_specs=spec,
        out_shape=jax.ShapeDtypeStruct(probes.shape, jnp.float32),
        cost_estimate=pl.CostEstimate(flops=2 * n * 256 * 8 * elements, bytes_accessed=8 * n * 4, transcendentals=0),
        name="evaluate",
    )(table, probes)

def split_rows(x):
    high = x.astype(jnp.bfloat16)
    rest = x - high.astype(jnp.float32)
    middle = rest.astype(jnp.bfloat16)
    low = (rest - middle.astype(jnp.float32)).astype(jnp.bfloat16)
    return jnp.concatenate([high, middle, low, jnp.zeros_like(low)], axis=0)

def join_rows(y):
    return y[0:8] + y[8:16] + y[16:24]

def ones_where(mask):
    return jnp.where(mask, jnp.ones(mask.shape, jnp.bfloat16), jnp.zeros(mask.shape, jnp.bfloat16))

def count_blocks(target_ref, place_ref, words_ref, picks_ref, sums_ref, ranks, tiles):
    blocks, _, rows = target_ref.shape
    ident = lax.broadcasted_iota(jnp.int32, (ranks, rows), 0)
    for k in range(blocks):
        mine = jnp.broadcast_to(target_ref[k], (ranks, rows)) == ident
        picks_ref[k * ranks:(k + 1) * ranks, :] = jnp.where(mine, 1.0, 0.0).astype(jnp.bfloat16)
    upper = lax.broadcasted_iota(jnp.int32, (rows, rows), 0) <= lax.broadcasted_iota(jnp.int32, (rows, rows), 1)
    upper = jnp.where(upper, 1.0, 0.0).astype(jnp.bfloat16)
    sums_ref[...] = jnp.dot(picks_ref[...], upper, preferred_element_type=jnp.float32)
    lane = lax.broadcasted_iota(jnp.int32, (ranks, LANES), 1)
    counts = jnp.zeros((ranks, LANES), jnp.float32)
    running = jnp.zeros((ranks, 1), jnp.float32)
    table = jnp.zeros((ranks, LANES), jnp.float32)
    for k in range(blocks):
        at = slice(k * ranks, (k + 1) * ranks)
        target = jnp.broadcast_to(target_ref[k], (ranks, rows))
        last = sums_ref[at, rows - 1:rows]
        before = jnp.where(ident < target, last, 0.0)
        placed = jnp.sum(jnp.where(target == ident, sums_ref[at, :], before), axis=0, keepdims=True) - 1.0
        place_ref[k:k + 1, :] = placed.astype(jnp.int32)
        table = jnp.where(lane == k, running, table)
        counts = jnp.where(lane == k, last, counts)
        running = running + last
    lower = lax.broadcasted_iota(jnp.int32, (ranks, ranks), 0) > lax.broadcasted_iota(jnp.int32, (ranks, ranks), 1)
    lower = jnp.where(lower, 1.0, 0.0).astype(jnp.bfloat16)
    high = jnp.floor(counts * 0.0625)
    parts = [jnp.dot(lower, c.astype(jnp.bfloat16), preferred_element_type=jnp.float32) for c in (high, counts - 16.0 * high)]
    offset = (16.0 * parts[0] + parts[1]).astype(jnp.int32)
    start = table.astype(jnp.int32)
    tile, low = lax.shift_right_logical(start, 7), start & (LANES - 1)
    rank = lax.broadcasted_iota(jnp.int32, (ranks, LANES), 0)
    send = ((rank * (tiles + 2) + tile) << 23) | (jnp.minimum(offset, rows - 1) << 14) | (low << 7) | ((low - offset) & (LANES - 1))
    cell = rank * tiles + jnp.minimum(tile, tiles - 1)
    take = (cell << 24) | (offset << 14) | (low << 7) | ((offset - low) & (LANES - 1))
    most = jnp.broadcast_to(jnp.max(counts, axis=0, keepdims=True).astype(jnp.int32), (8, LANES))
    words = jnp.concatenate([send, take, counts.astype(jnp.int32), most], axis=0)
    spare = -words.shape[0] % LANES
    words = jnp.concatenate([words, jnp.zeros((spare, LANES), jnp.int32)], axis=0)
    for c in range(0, words.shape[0], LANES):
        words_ref[:, c:c + LANES] = words[c:c + LANES, :].T[0:blocks]

def field(word, shift, mask):
    return lax.shift_right_logical(jnp.full((8, LANES), word, jnp.int32), shift) & mask

def window(lane, offset, pieces):
    mixed = pieces[-1]
    for i in range(len(pieces) - 2, -1, -1):
        mixed = jnp.where(lane + i * LANES >= offset, pieces[i], mixed)
    return mixed

def pack_kernel(target_ref, coordinates_ref, slot_ref, out_ref, place_ref, words_ref, picks_ref, sums_ref, buffer_ref, known_ref, semaphore, *, ranks, tiles, unroll):
    blocks, rows = place_ref.shape
    pieces = rows // LANES
    lane = lax.broadcasted_iota(jnp.int32, (8, LANES), 1)
    count_blocks(target_ref, place_ref, words_ref, picks_ref, sums_ref, ranks, tiles)
    copy = pltpu.make_async_copy(words_ref, known_ref, semaphore)
    copy.start()

    def clear(i, _):
        buffer_ref[i] = jnp.zeros((8, LANES), jnp.float32)
        return 0
    lax.fori_loop(0, ranks * (tiles + 2), clear, 0, unroll=16)
    copy.wait()
    across = lax.broadcasted_iota(jnp.int32, (rows, LANES), 1).astype(jnp.int16)

    def ordered(k, column):
        at = pl.ds(pl.multiple_of(k * rows, LANES), rows)
        payload = jnp.concatenate([coordinates_ref[:, at], slot_ref[k].astype(jnp.float32), jnp.zeros((4, rows), jnp.float32)], axis=0)
        column = jnp.broadcast_to(column, (rows, LANES)).astype(jnp.int16)
        hot = jnp.concatenate([ones_where(column == across + np.int16(i * LANES)) for i in range(pieces)], axis=1)
        block = join_rows(jnp.dot(split_rows(payload), hot, preferred_element_type=jnp.float32))
        return [block[:, i * LANES:(i + 1) * LANES] for i in range(pieces)]

    def main(g, _):
        columns = place_ref[pl.ds(pl.multiple_of(g * 8, 8), 8), :].T
        for u in range(8):
            k = g * 8 + u
            block = ordered(k, columns[:, u:u + 1])
            for r in range(0, ranks, unroll):
                moves = []
                for d in range(r, r + unroll):
                    word = known_ref[k, d]
                    moved = pltpu.roll(window(lane, field(word, 14, 511), block), word, 1)
                    cell = lax.shift_right_logical(word, 23)
                    moves.append((cell, moved, jnp.where(lane < field(word, 7, 127), buffer_ref[cell], moved)))
                for cell, moved, mixed in moves:
                    buffer_ref[cell] = mixed
                    buffer_ref[cell + 1] = moved
        return 0
    lax.fori_loop(0, blocks // 8, main, 0)

    def repair(k, _):
        @pl.when(known_ref[k, 3 * ranks] > LANES)
        def _():
            column = jnp.broadcast_to(place_ref[pl.ds(k, 1), :], (8, rows)).T[:, 0:1]
            block = ordered(k, column)
            for m in range(1, pieces):
                for d in range(ranks):
                    size = known_ref[k, 2 * ranks + d] - m * LANES
                    @pl.when(size > 0)
                    def _():
                        word = known_ref[k, d]
                        moved = pltpu.roll(window(lane, field(word, 14, 511), block[m:] + block[:1]), word, 1)
                        low = field(word, 7, 127)
                        high = low + jnp.minimum(size, LANES)
                        cell = lax.shift_right_logical(word, 23) + m
                        buffer_ref[cell] = jnp.where((lane >= low) & (lane < high), moved, buffer_ref[cell])
                        buffer_ref[cell + 1] = jnp.where(lane + LANES < high, moved, buffer_ref[cell + 1])
        return 0
    lax.fori_loop(0, blocks, repair, 0)

    for d in range(ranks):
        for t in range(tiles):
            out_ref[d, t] = buffer_ref[d * (tiles + 2) + t][0:4]

def pack(target, coordinates, slot, ranks, tiles, unroll=4):
    blocks, _, rows = target.shape
    table = (blocks, -(-(3 * ranks + 1) // LANES) * LANES)
    vm = pl.BlockSpec(memory_space=pltpu.VMEM)
    return pl.pallas_call(
        functools.partial(pack_kernel, ranks=ranks, tiles=tiles, unroll=unroll),
        in_specs=[vm] * 3,
        out_specs=(vm,) * 3,
        out_shape=(
            jax.ShapeDtypeStruct((ranks, tiles, 4, LANES), jnp.float32),
            jax.ShapeDtypeStruct((blocks, rows), jnp.int32),
            jax.ShapeDtypeStruct(table, jnp.int32),
        ),
        scratch_shapes=[
            pltpu.VMEM((blocks * ranks, rows), jnp.bfloat16),
            pltpu.VMEM((blocks * ranks, rows), jnp.float32),
            pltpu.VMEM((ranks * (tiles + 2), 8, LANES), jnp.float32),
            pltpu.SMEM(table, jnp.int32),
            pltpu.SemaphoreType.DMA,
        ],
        name="pack",
    )(target, coordinates, slot)

def unpack_kernel(known_ref, values_ref, place_ref, out_ref, held_ref, *, ranks, unroll):
    blocks, rows = place_ref.shape
    cells = values_ref.shape[0]
    pieces = rows // LANES
    lane = lax.broadcasted_iota(jnp.int32, (4, LANES), 1)
    down = lax.broadcasted_iota(jnp.int32, (rows, rows), 0).astype(jnp.int16)
    for i in range(cells):
        held_ref[i] = values_ref[i]
    held_ref[cells] = values_ref[0]

    def emit(k, row, whole):
        block = [jnp.zeros((4, LANES), jnp.float32)] * pieces
        for d in range(ranks):
            word = known_ref[k, ranks + d]
            cell = lax.shift_right_logical(word, 24)
            offset, low = field(word, 14, 1023)[0:4], field(word, 7, 127)[0:4]
            for m in range(pieces if whole else 1):
                at = [jnp.minimum(cell + m + i, cells) if m else cell + i for i in (0, 1)]
                moved = pltpu.roll(jnp.where(lane >= low, held_ref[at[0]], held_ref[at[1]]), word, 1)
                for i in range(m, pieces):
                    block[i] = jnp.where(lane + (i - m) * LANES >= offset, moved, block[i])
        block = jnp.concatenate(block, axis=1)
        block = jnp.concatenate([block, jnp.zeros_like(block)], axis=0)
        at = pl.ds(pl.multiple_of(k * rows, LANES), rows)
        hot = ones_where(jnp.broadcast_to(row, (rows, rows)).astype(jnp.int16) == down)
        out_ref[:, at] = join_rows(jnp.dot(split_rows(block), hot, preferred_element_type=jnp.float32))[0:4]

    def main(g, _):
        for u in range(unroll):
            k = g * unroll + u
            emit(k, place_ref[pl.ds(k, 1), :], False)
        return 0
    lax.fori_loop(0, blocks // unroll, main, 0)

    def repair(k, _):
        @pl.when(known_ref[k, 3 * ranks] > LANES)
        def _():
            emit(k, place_ref[pl.ds(k, 1), :], True)
        return 0
    lax.fori_loop(0, blocks, repair, 0)

def unpack(words, values, place, unroll=8):
    blocks, rows = place.shape
    ranks, tiles = values.shape[:2]
    vm = pl.BlockSpec(memory_space=pltpu.VMEM)
    return pl.pallas_call(
        functools.partial(unpack_kernel, ranks=ranks, unroll=unroll),
        in_specs=[pl.BlockSpec(memory_space=pltpu.SMEM), vm, vm],
        out_specs=vm,
        out_shape=jax.ShapeDtypeStruct((4, blocks * rows), jnp.float32),
        scratch_shapes=[pltpu.VMEM((ranks * tiles + 1, 4, LANES), jnp.float32)],
        name="unpack",
    )(words, values.reshape(ranks * tiles, 4, LANES), place)

def local(fields, coordinates, element_rank, element_slot):
    ranks = lax.axis_size(("gx", "gy", "gz"))
    probes = element_slot.shape[0]
    capacity = 5 * probes // (4 * ranks)
    tiles = -(-capacity // LANES)
    rows = math.gcd(probes, 512)
    target = element_rank.reshape(probes // rows, 1, rows)
    slot = element_slot.reshape(probes // rows, 1, rows)
    send, place, words = pack(target, coordinates, slot, ranks, tiles)
    arrived = lax.all_to_all(send, ("gx", "gy", "gz"), split_axis=0, concat_axis=0, tiled=True)
    values = evaluate(arrived.reshape(ranks * tiles, 4, LANES), fields).reshape(ranks, tiles, 4, LANES)
    returned = lax.all_to_all(values, ("gx", "gy", "gz"), split_axis=0, concat_axis=0, tiled=True)
    return unpack(words, returned, place)


def solution(mesh):
    placed = (
        P(("gx", "gy", "gz"), None),
        P(None, ("gx", "gy", "gz")),
        P(("gx", "gy", "gz"), None),
        P(("gx", "gy", "gz")),
    )
    return jax.shard_map(
        local, mesh=mesh, in_specs=placed, out_specs=P(None, ("gx", "gy", "gz")), check_vma=False
    )
```

profile of v0, /device:TPU:0, one launch (start us, length us, event | category | flops | bytes accessed | tf_op | source)
XLA Modules:
  0.0 69.2 jit_solution(5141477171781128308)
XLA Ops:
  0.0 0.0 copy-start
  0.0 12.6 %pack.1 = (f32[32,5,4,128]{3,2,1,0:T(4,128)}, s32[32,512]{1,0:T(8,128)}, s32[32,128]{1,0:T(8,128)}) custom-call(s32[32,1,512]{2,1,0:T(1,128)} %bitcast.14, f32[3,16384]{1,0:T(4,128)} %coordinates_ref.1, s32[32,1,512]{2,1,0:T(1,128)} %bitcast.15), custom_call_target="tpu_custom_call" | custom-call | tf_op jit(solution)/shard_map/pack/pallas_call | solution.py:206
  12.6 7.3 %all-to-all-start = ((f32[32,5,4,128]{3,2,1,0:T(4,128)}), f32[32,5,4,128]{3,2,1,0:T(4,128)S(1)}, u32[]{:S(2)}, u32[]{:S(2)}) async-start(f32[32,5,4,128]{3,2,1,0:T(4,128)} %get-tuple-element.9), calls=%async_computation | async-start | bytes 655360 | tf_op jit(solution)/shard_map/all_to_all | solution.py:288
  19.9 0.0 copy-done
  19.9 0.3 copy.6
  20.2 1.4 %copy.7 = bf16[4,8,8,8,128]{4,2,3,1,0:T(8,128)(2,1)} copy(bf16[4,8,8,8,128]{4,3,1,2,0:T(8,128)(2,1)S(1)} %bitcast.9) | data formatting | bytes 1048576 | tf_op jit(solution)/shard_map/transpose | solution.py:61
  21.6 10.3 %all-to-all-done = f32[32,5,4,128]{3,2,1,0:T(4,128)S(1)} async-done(((f32[32,5,4,128]{3,2,1,0:T(4,128)}), f32[32,5,4,128]{3,2,1,0:T(4,128)S(1)}, u32[]{:S(2)}, u32[]{:S(2)}) %all-to-all-start) | async-done | bytes 327712 | tf_op jit(solution)/shard_map/all_to_all | solution.py:288
  31.9 0.0 copy-start.1
  31.9 0.7 %copy-done.1 = f32[32,5,4,128]{3,2,1,0:T(4,128)} copy-done((f32[32,5,4,128]{3,2,1,0:T(4,128)}, f32[32,5,4,128]{3,2,1,0:T(4,128)S(1)}, u32[]{:S(2)}) %copy-start.1) | copy-done | bytes 327704
  32.7 14.1 %evaluate.1 = f32[160,4,128]{2,1,0:T(4,128)} custom-call(bf16[256,1024]{1,0:T(8,128)(2,1)} %bitcast.11, f32[160,4,128]{2,1,0:T(4,128)} %bitcast.12), custom_call_target="tpu_custom_call" | custom-call | flops 10737418240 | bytes 655360 | tf_op jit(solution)/shard_map/evaluate/pallas_call | solution.py:64
  46.7 15.3 %all_to_all.10 = f32[32,5,4,128]{3,2,1,0:T(4,128)} all-to-all(f32[32,5,4,128]{3,2,1,0:T(4,128)} %bitcast.13), channel_id=1, replica_groups=mesh['gx'=4,'gy'=4,'gz'=2] {'gx','gy','gz'}, dimensions={0} | all-to-all | bytes 655360 | tf_op jit(solution)/shard_map/all_to_all | solution.py:290
  62.0 7.1 %unpack.1 = f32[4,16384]{1,0:T(4,128)} custom-call(s32[32,128]{1,0:T(8,128)} %get-tuple-element.8.known_ref, f32[160,4,128]{2,1,0:T(4,128)} %bitcast.10, s32[32,512]{1,0:T(8,128)} %get-tuple-element.10.place_ref), custom_call_target="tpu_custom_call" | custom-call | tf_op jit(solution)/shard_map/unpack/pallas_call | solution.py:270
Async XLA Ops:
  0.0 19.9 %copy-start = (bf16[128,2048]{1,0:T(8,128)(2,1)S(1)}, bf16[128,2048]{1,0:T(8,128)(2,1)}, u32[]{:S(2)}) copy-start(bf16[128,2048]{1,0:T(8,128)(2,1)} %param.4) | copy-start | bytes 1572868
  12.6 19.4 %all-to-all-start = ((f32[32,5,4,128]{3,2,1,0:T(4,128)}), f32[32,5,4,128]{3,2,1,0:T(4,128)S(1)}, u32[]{:S(2)}, u32[]{:S(2)}) async-start(f32[32,5,4,128]{3,2,1,0:T(4,128)} %get-tuple-element.9), calls=%async_computation | async-start | bytes 655360 | tf_op jit(solution)/shard_map/all_to_all | solution.py:288
  31.9 0.7 %copy-start.1 = (f32[32,5,4,128]{3,2,1,0:T(4,128)}, f32[32,5,4,128]{3,2,1,0:T(4,128)S(1)}, u32[]{:S(2)}) copy-start(f32[32,5,4,128]{3,2,1,0:T(4,128)S(1)} %all-to-all-done) | copy-start | bytes 983044
where the time goes:
time: 69.5 us; the launch traced here: 69.2 us
  Pallas kernels  33.7 us (48%)
  blocking collectives  15.3 us (22%)
  waiting for transfers between devices  10.3 us (15%)
  starting transfers between devices  7.33 us (11%)
  local copies, waits for them, and re-layouts  2.43 us (3%)
    all_to_all x1, blocking collectives, local(): lax.all_to_all(values, ('gx', 'gy', 'gz'), split_axis=0, concat_axis=0, t...  15.3 us
    pallas_call x1, Pallas kernels, evaluate(): pl.pallas_call(functools.partial(evaluate_kernel, step=step), grid=(parts...  14.1 us
    pallas_call x1, Pallas kernels, pack(): pl.pallas_call(functools.partial(pack_kernel, ranks=ranks, tiles=tiles, u...  12.6 us
    all_to_all x1, waiting for transfers between devices, local(): lax.all_to_all(send, ('gx', 'gy', 'gz'), split_axis=0, concat_axis=0, til...  10.3 us
    all_to_all x1, starting transfers between devices, local(): lax.all_to_all(send, ('gx', 'gy', 'gz'), split_axis=0, concat_axis=0, til...  7.33 us
    pallas_call x1, Pallas kernels, unpack(): pl.pallas_call(functools.partial(unpack_kernel, ranks=ranks, unroll=unrol...  7.13 us
    transpose x1, local copies, waits for them, and re-layouts, evaluate(): fields.reshape(elements, 4, 8, 8, 8).transpose(1, 3, 2, 4, 0)  1.42 us
  transfers between devices with their start and end apart: 1, of which 1 were waited for; matrix products, arithmetic and copies ran while one was open for 2% of the time, Pallas kernels for 0%

commit v1 on v0

--- a/solution.py
+++ b/solution.py
@@ -68,6 +68,7 @@
         out_specs=spec,
         out_shape=jax.ShapeDtypeStruct(probes.shape, jnp.float32),
         cost_estimate=pl.CostEstimate(flops=2 * n * 256 * 8 * elements, bytes_accessed=8 * n * 4, transcendentals=0),
+        compiler_params=pltpu.CompilerParams(vmem_limit_bytes=16 << 20),
         name="evaluate",
     )(table, probes)
 
@@ -118,28 +119,38 @@
     send = ((rank * (tiles + 2) + tile) << 23) | (jnp.minimum(offset, rows - 1) << 14) | (low << 7) | ((low - offset) & (LANES - 1))
     cell = rank * tiles + jnp.minimum(tile, tiles - 1)
     take = (cell << 24) | (offset << 14) | (low << 7) | ((offset - low) & (LANES - 1))
-    most = jnp.broadcast_to(jnp.max(counts, axis=0, keepdims=True).astype(jnp.int32), (8, LANES))
+    most = jnp.max(counts, axis=0, keepdims=True)
+    peak = jnp.broadcast_to(jnp.max(most, axis=1, keepdims=True), most.shape)
+    most = jnp.concatenate([most, peak, jnp.zeros((6, LANES), jnp.float32)], axis=0).astype(jnp.int32)
     words = jnp.concatenate([send, take, counts.astype(jnp.int32), most], axis=0)
     spare = -words.shape[0] % LANES
     words = jnp.concatenate([words, jnp.zeros((spare, LANES), jnp.int32)], axis=0)
     for c in range(0, words.shape[0], LANES):
         words_ref[:, c:c + LANES] = words[c:c + LANES, :].T[0:blocks]
 
-def field(word, shift, mask):
-    return lax.shift_right_logical(jnp.full((8, LANES), word, jnp.int32), shift) & mask
+def reach(lane, shift, i=0):
+    return ((lane + i * LANES) << shift) | ((1 << shift) - 1)
 
 def window(lane, offset, pieces):
     mixed = pieces[-1]
     for i in range(len(pieces) - 2, -1, -1):
-        mixed = jnp.where(lane + i * LANES >= offset, pieces[i], mixed)
+        mixed = jnp.where(reach(lane, 14, i) >= offset, pieces[i], mixed)
     return mixed
 
-def pack_kernel(target_ref, coordinates_ref, slot_ref, out_ref, place_ref, words_ref, picks_ref, sums_ref, buffer_ref, known_ref, semaphore, *, ranks, tiles, unroll):
+def pack_kernel(target_hbm, coordinates_hbm, slot_hbm, out_ref, place_ref, words_ref, target_ref, coordinates_ref, slot_ref, picks_ref, sums_ref, buffer_ref, known_ref, semaphores, *, ranks, tiles, unroll):
     blocks, rows = place_ref.shape
     pieces = rows // LANES
     lane = lax.broadcasted_iota(jnp.int32, (8, LANES), 1)
+    fetches = [
+        pltpu.make_async_copy(target_hbm, target_ref, semaphores.at[0]),
+        pltpu.make_async_copy(coordinates_hbm, coordinates_ref, semaphores.at[1]),
+        pltpu.make_async_copy(slot_hbm, slot_ref, semaphores.at[2]),
+    ]
+    for fetch in fetches:
+        fetch.start()
+    fetches[0].wait()
     count_blocks(target_ref, place_ref, words_ref, picks_ref, sums_ref, ranks, tiles)
-    copy = pltpu.make_async_copy(words_ref, known_ref, semaphore)
+    copy = pltpu.make_async_copy(words_ref, known_ref, semaphores.at[3])
     copy.start()
 
     def clear(i, _):
@@ -147,30 +158,30 @@
         return 0
     lax.fori_loop(0, ranks * (tiles + 2), clear, 0, unroll=16)
     copy.wait()
-    across = lax.broadcasted_iota(jnp.int32, (rows, LANES), 1).astype(jnp.int16)
-
-    def ordered(k, column):
+    for fetch in fetches[1:]:
+        fetch.wait()
+    down = lax.broadcasted_iota(jnp.int32, (rows, rows), 0).astype(jnp.int16)
+
+    def ordered(k):
         at = pl.ds(pl.multiple_of(k * rows, LANES), rows)
         payload = jnp.concatenate([coordinates_ref[:, at], slot_ref[k].astype(jnp.float32), jnp.zeros((4, rows), jnp.float32)], axis=0)
-        column = jnp.broadcast_to(column, (rows, LANES)).astype(jnp.int16)
-        hot = jnp.concatenate([ones_where(column == across + np.int16(i * LANES)) for i in range(pieces)], axis=1)
-        block = join_rows(jnp.dot(split_rows(payload), hot, preferred_element_type=jnp.float32))
+        hot = ones_where(jnp.broadcast_to(place_ref[pl.ds(k, 1), :], (rows, rows)).astype(jnp.int16) == down)
+        block = join_rows(lax.dot_general(split_rows(payload), hot, (((1,), (1,)), ((), ())), preferred_element_type=jnp.float32))
         return [block[:, i * LANES:(i + 1) * LANES] for i in range(pieces)]
 
     def main(g, _):
-        columns = place_ref[pl.ds(pl.multiple_of(g * 8, 8), 8), :].T
         for u in range(8):
             k = g * 8 + u
-            block = ordered(k, columns[:, u:u + 1])
+            block = ordered(k)
             for r in range(0, ranks, unroll):
                 moves = []
                 for d in range(r, r + unroll):
                     word = known_ref[k, d]
-                    moved = pltpu.roll(window(lane, field(word, 14, 511), block), word, 1)
-                    cell = lax.shift_right_logical(word, 23)
-                    moves.append((cell, moved, jnp.where(lane < field(word, 7, 127), buffer_ref[cell], moved)))
-                for cell, moved, mixed in moves:
-                    buffer_ref[cell] = mixed
+                    wide = jnp.full((8, LANES), word, jnp.int32)
+                    moved = pltpu.roll(window(lane, wide & ((1 << 23) - 1), block), word, 1)
+                    moves.append((lax.shift_right_logical(word, 23), moved, reach(lane, 7) >= (wide & ((1 << 14) - 1))))
+                for cell, moved, mask in moves:
+                    pltpu.store(buffer_ref.at[cell], moved, mask=mask)
                     buffer_ref[cell + 1] = moved
         return 0
     lax.fori_loop(0, blocks // 8, main, 0)
@@ -178,22 +189,24 @@
     def repair(k, _):
         @pl.when(known_ref[k, 3 * ranks] > LANES)
         def _():
-            column = jnp.broadcast_to(place_ref[pl.ds(k, 1), :], (8, rows)).T[:, 0:1]
-            block = ordered(k, column)
+            block = ordered(k)
             for m in range(1, pieces):
                 for d in range(ranks):
                     size = known_ref[k, 2 * ranks + d] - m * LANES
                     @pl.when(size > 0)
                     def _():
                         word = known_ref[k, d]
-                        moved = pltpu.roll(window(lane, field(word, 14, 511), block[m:] + block[:1]), word, 1)
-                        low = field(word, 7, 127)
+                        moved = pltpu.roll(window(lane, word & ((1 << 23) - 1), block[m:] + block[:1]), word, 1)
+                        low = lax.shift_right_logical(word, 7) & (LANES - 1)
                         high = low + jnp.minimum(size, LANES)
                         cell = lax.shift_right_logical(word, 23) + m
                         buffer_ref[cell] = jnp.where((lane >= low) & (lane < high), moved, buffer_ref[cell])
                         buffer_ref[cell + 1] = jnp.where(lane + LANES < high, moved, buffer_ref[cell + 1])
         return 0
-    lax.fori_loop(0, blocks, repair, 0)
+
+    @pl.when(known_ref[0, 3 * ranks + 1] > LANES)
+    def _():
+        lax.fori_loop(0, blocks, repair, 0)
 
     for d in range(ranks):
         for t in range(tiles):
@@ -201,11 +214,11 @@
 
 def pack(target, coordinates, slot, ranks, tiles, unroll=4):
     blocks, _, rows = target.shape
-    table = (blocks, -(-(3 * ranks + 1) // LANES) * LANES)
+    table = (blocks, -(-(3 * ranks + 2) // LANES) * LANES)
     vm = pl.BlockSpec(memory_space=pltpu.VMEM)
     return pl.pallas_call(
         functools.partial(pack_kernel, ranks=ranks, tiles=tiles, unroll=unroll),
-        in_specs=[vm] * 3,
+        in_specs=[pl.BlockSpec(memory_space=pltpu.HBM)] * 3,
         out_specs=(vm,) * 3,
         out_shape=(
             jax.ShapeDtypeStruct((ranks, tiles, 4, LANES), jnp.float32),
@@ -213,12 +226,16 @@
             jax.ShapeDtypeStruct(table, jnp.int32),
         ),
         scratch_shapes=[
+            pltpu.VMEM(target.shape, jnp.int32),
+            pltpu.VMEM(coordinates.shape, jnp.float32),
+            pltpu.VMEM(slot.shape, jnp.int32),
             pltpu.VMEM((blocks * ranks, rows), jnp.bfloat16),
             pltpu.VMEM((blocks * ranks, rows), jnp.float32),
             pltpu.VMEM((ranks * (tiles + 2), 8, LANES), jnp.float32),
             pltpu.SMEM(table, jnp.int32),
-            pltpu.SemaphoreType.DMA,
+            pltpu.SemaphoreType.DMA((4,)),
         ],
+        compiler_params=pltpu.CompilerParams(vmem_limit_bytes=60 << 20),
         name="pack",
     )(target, coordinates, slot)
 
@@ -237,12 +254,13 @@
         for d in range(ranks):
             word = known_ref[k, ranks + d]
             cell = lax.shift_right_logical(word, 24)
-            offset, low = field(word, 14, 1023)[0:4], field(word, 7, 127)[0:4]
+            wide = jnp.full((4, LANES), word, jnp.int32)
+            offset, low = wide & ((1 << 24) - 1), wide & ((1 << 14) - 1)
             for m in range(pieces if whole else 1):
                 at = [jnp.minimum(cell + m + i, cells) if m else cell + i for i in (0, 1)]
-                moved = pltpu.roll(jnp.where(lane >= low, held_ref[at[0]], held_ref[at[1]]), word, 1)
+                moved = pltpu.roll(jnp.where(reach(lane, 7) >= low, held_ref[at[0]], held_ref[at[1]]), word, 1)
                 for i in range(m, pieces):
-                    block[i] = jnp.where(lane + (i - m) * LANES >= offset, moved, block[i])
+                    block[i] = jnp.where(reach(lane, 14, i - m) >= offset, moved, block[i])
         block = jnp.concatenate(block, axis=1)
         block = jnp.concatenate([block, jnp.zeros_like(block)], axis=0)
         at = pl.ds(pl.multiple_of(k * rows, LANES), rows)
@@ -261,7 +279,10 @@
         def _():
             emit(k, place_ref[pl.ds(k, 1), :], True)
         return 0
-    lax.fori_loop(0, blocks, repair, 0)
+
+    @pl.when(known_ref[0, 3 * ranks + 1] > LANES)
+    def _():
+        lax.fori_loop(0, blocks, repair, 0)
 
 def unpack(words, values, place, unroll=8):
     blocks, rows = place.shape
@@ -273,6 +294,7 @@
         out_specs=vm,
         out_shape=jax.ShapeDtypeStruct((4, blocks * rows), jnp.float32),
         scratch_shapes=[pltpu.VMEM((ranks * tiles + 1, 4, LANES), jnp.float32)],
+        compiler_params=pltpu.CompilerParams(vmem_limit_bytes=8 << 20),
         name="unpack",
     )(words, values.reshape(ranks * tiles, 4, LANES), place)
 

time: 69.5 us -> 62 us (0.89)
  Pallas kernels: 33.7 us -> 28.3 us
  local copies, waits for them, and re-layouts: 2.43 us -> 0.9 us
  blocking collectives: 15.3 us -> 14.1 us
  waiting for transfers between devices: 10.3 us -> 11.1 us
    pallas_call x1, Pallas kernels: 12.6 us -> 10.2 us  [pack(): pl.pallas_call(functools.partial(pack_kernel, ranks=ranks, tiles=tiles, u...]
    pallas_call x1, Pallas kernels: 14.1 us -> 12.3 us  [evaluate(): pl.pallas_call(functools.partial(evaluate_kernel, step=step), grid=(parts...]
    pallas_call x1, Pallas kernels: 7.13 us -> 5.82 us  [unpack(): pl.pallas_call(functools.partial(unpack_kernel, ranks=ranks, unroll=unrol...]
    all_to_all x1, blocking collectives: 15.3 us -> 14.1 us  [local(): lax.all_to_all(values, ('gx', 'gy', 'gz'), split_axis=0, concat_axis=0, t...]
    transpose x1, local copies, waits for them, and re-layouts: 1.42 us -> 0.62 us  [evaluate(): fields.reshape(elements, 4, 8, 8, 8).transpose(1, 3, 2, 4, 0)]
    all_to_all x1, waiting for transfers between devices: 10.3 us -> 11.1 us  [local(): lax.all_to_all(send, ('gx', 'gy', 'gz'), split_axis=0, concat_axis=0, til...]
    unnamed x5 -> x7, local copies, waits for them, and re-layouts: 1.01 us -> 0.28 us
  transfers between devices with their start and end apart: 1 -> 1, of which waited for: 1 -> 1; matrix products, arithmetic and copies ran while one was open for 2% -> 1% of each run, Pallas kernels for 0% -> 0%
where the time goes in v1:
time: 62 us; the launch traced here: 61.7 us
  Pallas kernels  28.3 us (46%)
  blocking collectives  14.1 us (23%)
  waiting for transfers between devices  11.1 us (18%)
  starting transfers between devices  7.33 us (12%)
  local copies, waits for them, and re-layouts  0.9 us (1%)
    all_to_all x1, blocking collectives, local(): lax.all_to_all(values, ('gx', 'gy', 'gz'), split_axis=0, concat_axis=0, t...  14.1 us
    pallas_call x1, Pallas kernels, evaluate(): pl.pallas_call(functools.partial(evaluate_kernel, step=step), grid=(parts...  12.3 us
    all_to_all x1, waiting for transfers between devices, local(): lax.all_to_all(send, ('gx', 'gy', 'gz'), split_axis=0, concat_axis=0, til...  11.1 us
    pallas_call x1, Pallas kernels, pack(): pl.pallas_call(functools.partial(pack_kernel, ranks=ranks, tiles=tiles, u...  10.2 us
    all_to_all x1, starting transfers between devices, local(): lax.all_to_all(send, ('gx', 'gy', 'gz'), split_axis=0, concat_axis=0, til...  7.33 us
    pallas_call x1, Pallas kernels, unpack(): pl.pallas_call(functools.partial(unpack_kernel, ranks=ranks, unroll=unrol...  5.82 us
  transfers between devices with their start and end apart: 1, of which 1 were waited for; matrix products, arithmetic and copies ran while one was open for 1% of the time, Pallas kernels for 0%

profile of v1, /device:TPU:0, one launch (start us, length us, event | category | flops | bytes accessed | tf_op | source)
XLA Modules:
  0.0 61.7 jit_solution(6486574333623022173)
XLA Ops:
  0.0 0.0 copy-start.2
  0.0 10.2 %pack.1 = (f32[32,5,4,128]{3,2,1,0:T(4,128)}, s32[32,512]{1,0:T(8,128)}, s32[32,128]{1,0:T(8,128)}) custom-call(s32[32,1,512]{2,1,0:T(1,128)} %bitcast.14, f32[3,16384]{1,0:T(4,128)} %coordinates_hbm.1, s32[32,1,512]{2,1,0:T(1,128)} %bitcast.15), custom_call_target="tpu_custom_call" | custom-call | tf_op jit(solution)/shard_map/pack/pallas_call | solution.py:219
  10.2 7.3 %all-to-all-start = ((f32[32,5,4,128]{3,2,1,0:T(4,128)}), f32[32,5,4,128]{3,2,1,0:T(4,128)S(1)}, u32[]{:S(2)}, u32[]{:S(2)}) async-start(f32[32,5,4,128]{3,2,1,0:T(4,128)} %get-tuple-element.9), calls=%async_computation | async-start | bytes 655360 | tf_op jit(solution)/shard_map/all_to_all | solution.py:310
  17.5 0.0 copy-done.2
  17.5 0.3 copy.6
  17.8 0.6 copy.7
  18.4 11.1 %all-to-all-done = f32[32,5,4,128]{3,2,1,0:T(4,128)S(1)} async-done(((f32[32,5,4,128]{3,2,1,0:T(4,128)}), f32[32,5,4,128]{3,2,1,0:T(4,128)S(1)}, u32[]{:S(2)}, u32[]{:S(2)}) %all-to-all-start) | async-done | bytes 327712 | tf_op jit(solution)/shard_map/all_to_all | solution.py:310
  29.5 12.3 %evaluate.1 = f32[160,4,128]{2,1,0:T(4,128)S(1)} custom-call(bf16[256,1024]{1,0:T(8,128)(2,1)S(1)} %bitcast.10, f32[160,4,128]{2,1,0:T(4,128)S(1)} %bitcast.11), custom_call_target="tpu_custom_call" | custom-call | flops 10737418240 | bytes 655360 | tf_op jit(solution)/shard_map/evaluate/pallas_call | solution.py:64
  41.8 0.0 copy-start
  41.8 0.0 copy-start.1
  41.8 14.1 %all_to_all.10 = f32[32,5,4,128]{3,2,1,0:T(4,128)S(1)} all-to-all(f32[32,5,4,128]{3,2,1,0:T(4,128)S(1)} %bitcast.12), channel_id=1, replica_groups=mesh['gx'=4,'gy'=4,'gz'=2] {'gx','gy','gz'}, dimensions={0} | all-to-all | bytes 655360 | tf_op jit(solution)/shard_map/all_to_all | solution.py:312
  55.9 0.0 copy-done
  55.9 0.0 copy-done.1
  55.9 5.8 %unpack.1 = f32[4,16384]{1,0:T(4,128)} custom-call(s32[32,128]{1,0:T(8,128)S(1)} %copy-done.1, f32[160,4,128]{2,1,0:T(4,128)S(1)} %bitcast.9, s32[32,512]{1,0:T(8,128)S(1)} %copy-done), custom_call_target="tpu_custom_call" | custom-call | tf_op jit(solution)/shard_map/unpack/pallas_call | solution.py:291
Async XLA Ops:
  0.0 17.5 %copy-start.2 = (bf16[128,2048]{1,0:T(8,128)(2,1)S(1)}, bf16[128,2048]{1,0:T(8,128)(2,1)}, u32[]{:S(2)}) copy-start(bf16[128,2048]{1,0:T(8,128)(2,1)} %param.4) | copy-start | bytes 1572868
  10.2 19.4 %all-to-all-start = ((f32[32,5,4,128]{3,2,1,0:T(4,128)}), f32[32,5,4,128]{3,2,1,0:T(4,128)S(1)}, u32[]{:S(2)}, u32[]{:S(2)}) async-start(f32[32,5,4,128]{3,2,1,0:T(4,128)} %get-tuple-element.9), calls=%async_computation | async-start | bytes 655360 | tf_op jit(solution)/shard_map/all_to_all | solution.py:310
  41.8 14.1 %copy-start = (s32[32,512]{1,0:T(8,128)S(1)}, s32[32,512]{1,0:T(8,128)}, u32[]{:S(2)}) copy-start(s32[32,512]{1,0:T(8,128)} %get-tuple-element.10.place_ref) | copy-start | bytes 196612
  41.8 14.1 %copy-start.1 = (s32[32,128]{1,0:T(8,128)S(1)}, s32[32,128]{1,0:T(8,128)}, u32[]{:S(2)}) copy-start(s32[32,128]{1,0:T(8,128)} %get-tuple-element.8.known_ref) | copy-start | bytes 49156

commit v2 on v1

--- a/solution.py
+++ b/solution.py
@@ -128,6 +128,15 @@
     for c in range(0, words.shape[0], LANES):
         words_ref[:, c:c + LANES] = words[c:c + LANES, :].T[0:blocks]
 
+def span_of(blocks, ranks):
+    return math.gcd(blocks, max(1, 1024 // ranks))
+
+def for_blocks(blocks, span, body):
+    if span == blocks:
+        body(0, 0)
+    else:
+        lax.fori_loop(0, blocks // span, body, 0)
+
 def reach(lane, shift, i=0):
     return ((lane + i * LANES) << shift) | ((1 << shift) - 1)
 
@@ -137,7 +146,7 @@
         mixed = jnp.where(reach(lane, 14, i) >= offset, pieces[i], mixed)
     return mixed
 
-def pack_kernel(target_hbm, coordinates_hbm, slot_hbm, out_ref, place_ref, words_ref, target_ref, coordinates_ref, slot_ref, picks_ref, sums_ref, buffer_ref, known_ref, semaphores, *, ranks, tiles, unroll):
+def pack_kernel(target_hbm, coordinates_hbm, slot_hbm, out_ref, place_ref, words_ref, target_ref, coordinates_ref, slot_ref, picks_ref, sums_ref, buffer_ref, known_ref, semaphores, *, ranks, tiles, unroll, span):
     blocks, rows = place_ref.shape
     pieces = rows // LANES
     lane = lax.broadcasted_iota(jnp.int32, (8, LANES), 1)
@@ -169,22 +178,24 @@
         block = join_rows(lax.dot_general(split_rows(payload), hot, (((1,), (1,)), ((), ())), preferred_element_type=jnp.float32))
         return [block[:, i * LANES:(i + 1) * LANES] for i in range(pieces)]
 
+    def spread(k, block):
+        for r in range(0, ranks, unroll):
+            moves = []
+            for d in range(r, r + unroll):
+                word = known_ref[k, d]
+                wide = jnp.full((8, LANES), word, jnp.int32)
+                moved = pltpu.roll(window(lane, wide & ((1 << 23) - 1), block), word, 1)
+                moves.append((lax.shift_right_logical(word, 23), moved, reach(lane, 7) >= (wide & ((1 << 14) - 1))))
+            for cell, moved, mask in moves:
+                pltpu.store(buffer_ref.at[cell], moved, mask=mask)
+                buffer_ref[cell + 1] = moved
+
     def main(g, _):
-        for u in range(8):
-            k = g * 8 + u
-            block = ordered(k)
-            for r in range(0, ranks, unroll):
-                moves = []
-                for d in range(r, r + unroll):
-                    word = known_ref[k, d]
-                    wide = jnp.full((8, LANES), word, jnp.int32)
-                    moved = pltpu.roll(window(lane, wide & ((1 << 23) - 1), block), word, 1)
-                    moves.append((lax.shift_right_logical(word, 23), moved, reach(lane, 7) >= (wide & ((1 << 14) - 1))))
-                for cell, moved, mask in moves:
-                    pltpu.store(buffer_ref.at[cell], moved, mask=mask)
-                    buffer_ref[cell + 1] = moved
-        return 0
-    lax.fori_loop(0, blocks // 8, main, 0)
+        for u in range(span):
+            k = g * span + u
+            spread(k, ordered(k))
+        return 0
+    for_blocks(blocks, span, main)
 
     def repair(k, _):
         @pl.when(known_ref[k, 3 * ranks] > LANES)
@@ -217,7 +228,7 @@
     table = (blocks, -(-(3 * ranks + 2) // LANES) * LANES)
     vm = pl.BlockSpec(memory_space=pltpu.VMEM)
     return pl.pallas_call(
-        functools.partial(pack_kernel, ranks=ranks, tiles=tiles, unroll=unroll),
+        functools.partial(pack_kernel, ranks=ranks, tiles=tiles, unroll=unroll, span=span_of(blocks, ranks)),
         in_specs=[pl.BlockSpec(memory_space=pltpu.HBM)] * 3,
         out_specs=(vm,) * 3,
         out_shape=(
@@ -272,7 +283,7 @@
             k = g * unroll + u
             emit(k, place_ref[pl.ds(k, 1), :], False)
         return 0
-    lax.fori_loop(0, blocks // unroll, main, 0)
+    for_blocks(blocks, unroll, main)
 
     def repair(k, _):
         @pl.when(known_ref[k, 3 * ranks] > LANES)
@@ -284,12 +295,12 @@
     def _():
         lax.fori_loop(0, blocks, repair, 0)
 
-def unpack(words, values, place, unroll=8):
+def unpack(words, values, place):
     blocks, rows = place.shape
     ranks, tiles = values.shape[:2]
     vm = pl.BlockSpec(memory_space=pltpu.VMEM)
     return pl.pallas_call(
-        functools.partial(unpack_kernel, ranks=ranks, unroll=unroll),
+        functools.partial(unpack_kernel, ranks=ranks, unroll=span_of(blocks, ranks)),
         in_specs=[pl.BlockSpec(memory_space=pltpu.SMEM), vm, vm],
         out_specs=vm,
         out_shape=jax.ShapeDtypeStruct((4, blocks * rows), jnp.float32),

time: 62 us -> 60.8 us (0.981)
  Pallas kernels: 28.3 us -> 27.1 us
where the time goes in v2:
time: 60.8 us; the launch traced here: 60.6 us
  Pallas kernels  27.1 us (45%)
  blocking collectives  14.1 us (23%)
  waiting for transfers between devices  10.9 us (18%)
  starting transfers between devices  7.52 us (12%)
  local copies, waits for them, and re-layouts  0.9 us (1%)
    all_to_all x1, blocking collectives, local(): lax.all_to_all(values, ('gx', 'gy', 'gz'), split_axis=0, concat_axis=0, t...  14.1 us
    pallas_call x1, Pallas kernels, evaluate(): pl.pallas_call(functools.partial(evaluate_kernel, step=step), grid=(parts...  12.3 us
    all_to_all x1, waiting for transfers between devices, local(): lax.all_to_all(send, ('gx', 'gy', 'gz'), split_axis=0, concat_axis=0, til...  10.9 us
    pallas_call x1, Pallas kernels, pack(): pl.pallas_call(functools.partial(pack_kernel, ranks=ranks, tiles=tiles, u...  9.55 us
    all_to_all x1, starting transfers between devices, local(): lax.all_to_all(send, ('gx', 'gy', 'gz'), split_axis=0, concat_axis=0, til...  7.52 us
    pallas_call x1, Pallas kernels, unpack(): pl.pallas_call(functools.partial(unpack_kernel, ranks=ranks, unroll=span_...  5.27 us
  transfers between devices with their start and end apart: 1, of which 1 were waited for; matrix products, arithmetic and copies ran while one was open for 1% of the time, Pallas kernels for 0%

profile of v2, /device:TPU:0, one launch (start us, length us, event | category | flops | bytes accessed | tf_op | source)
XLA Modules:
  0.0 60.6 jit_solution(9306935871428592173)
XLA Ops:
  0.0 0.0 copy-start.2
  0.0 9.6 %pack.1 = (f32[32,5,4,128]{3,2,1,0:T(4,128)}, s32[32,512]{1,0:T(8,128)}, s32[32,128]{1,0:T(8,128)}) custom-call(s32[32,1,512]{2,1,0:T(1,128)} %bitcast.14, f32[3,16384]{1,0:T(4,128)} %coordinates_hbm.1, s32[32,1,512]{2,1,0:T(1,128)} %bitcast.15), custom_call_target="tpu_custom_call" | custom-call | tf_op jit(solution)/shard_map/pack/pallas_call | solution.py:230
  9.6 7.5 %all-to-all-start = ((f32[32,5,4,128]{3,2,1,0:T(4,128)}), f32[32,5,4,128]{3,2,1,0:T(4,128)S(1)}, u32[]{:S(2)}, u32[]{:S(2)}) async-start(f32[32,5,4,128]{3,2,1,0:T(4,128)} %get-tuple-element.9), calls=%async_computation | async-start | bytes 655360 | tf_op jit(solution)/shard_map/all_to_all | solution.py:321
  17.1 0.0 copy-done.2
  17.1 0.3 copy.6
  17.4 0.6 %copy.7 = bf16[4,8,8,8,128]{4,2,3,1,0:T(8,128)(2,1)S(1)} copy(bf16[4,8,8,8,128]{4,3,1,2,0:T(8,128)(2,1)S(1)} %bitcast.13) | data formatting | bytes 1048576 | tf_op jit(solution)/shard_map/transpose | solution.py:61
  18.0 10.9 %all-to-all-done = f32[32,5,4,128]{3,2,1,0:T(4,128)S(1)} async-done(((f32[32,5,4,128]{3,2,1,0:T(4,128)}), f32[32,5,4,128]{3,2,1,0:T(4,128)S(1)}, u32[]{:S(2)}, u32[]{:S(2)}) %all-to-all-start) | async-done | bytes 327712 | tf_op jit(solution)/shard_map/all_to_all | solution.py:321
  28.9 12.3 %evaluate.1 = f32[160,4,128]{2,1,0:T(4,128)S(1)} custom-call(bf16[256,1024]{1,0:T(8,128)(2,1)S(1)} %bitcast.10, f32[160,4,128]{2,1,0:T(4,128)S(1)} %bitcast.11), custom_call_target="tpu_custom_call" | custom-call | flops 10737418240 | bytes 655360 | tf_op jit(solution)/shard_map/evaluate/pallas_call | solution.py:64
  41.2 0.0 copy-start
  41.2 0.0 copy-start.1
  41.2 14.1 %all_to_all.10 = f32[32,5,4,128]{3,2,1,0:T(4,128)S(1)} all-to-all(f32[32,5,4,128]{3,2,1,0:T(4,128)S(1)} %bitcast.12), channel_id=1, replica_groups=mesh['gx'=4,'gy'=4,'gz'=2] {'gx','gy','gz'}, dimensions={0} | all-to-all | bytes 655360 | tf_op jit(solution)/shard_map/all_to_all | solution.py:323
  55.3 0.0 copy-done
  55.3 0.0 copy-done.1
  55.3 5.3 %unpack.1 = f32[4,16384]{1,0:T(4,128)} custom-call(s32[32,128]{1,0:T(8,128)S(1)} %copy-done.1, f32[160,4,128]{2,1,0:T(4,128)S(1)} %bitcast.9, s32[32,512]{1,0:T(8,128)S(1)} %copy-done), custom_call_target="tpu_custom_call" | custom-call | tf_op jit(solution)/shard_map/unpack/pallas_call | solution.py:302
Async XLA Ops:
  0.0 17.1 %copy-start.2 = (bf16[128,2048]{1,0:T(8,128)(2,1)S(1)}, bf16[128,2048]{1,0:T(8,128)(2,1)}, u32[]{:S(2)}) copy-start(bf16[128,2048]{1,0:T(8,128)(2,1)} %param.4) | copy-start | bytes 1572868
  9.6 19.4 %all-to-all-start = ((f32[32,5,4,128]{3,2,1,0:T(4,128)}), f32[32,5,4,128]{3,2,1,0:T(4,128)S(1)}, u32[]{:S(2)}, u32[]{:S(2)}) async-start(f32[32,5,4,128]{3,2,1,0:T(4,128)} %get-tuple-element.9), calls=%async_computation | async-start | bytes 655360 | tf_op jit(solution)/shard_map/all_to_all | solution.py:321
  41.2 14.1 %copy-start = (s32[32,512]{1,0:T(8,128)S(1)}, s32[32,512]{1,0:T(8,128)}, u32[]{:S(2)}) copy-start(s32[32,512]{1,0:T(8,128)} %get-tuple-element.10.place_ref) | copy-start | bytes 196612
  41.2 14.1 %copy-start.1 = (s32[32,128]{1,0:T(8,128)S(1)}, s32[32,128]{1,0:T(8,128)}, u32[]{:S(2)}) copy-start(s32[32,128]{1,0:T(8,128)} %get-tuple-element.8.known_ref) | copy-start | bytes 49156
